TPU v7x, 32 devices: a whole 2x2x4 slice. The times are simulated.
32 devices in a mesh: ctx: 8 (over z, x), fsdp: 4 (over y, core).
Axes of the slice: x: 2, y: 2, z: 4, core: 2. Of those that a mesh axis runs over, the one named last changes fastest.
Arguments:
- tokens: bfloat16 [8, 2, 256, 1536], P('ctx', None, 'fsdp'), may hold values from -6 to 6
- pairing: int32 [8], replicated, may hold values from 0 to 7, each once
- gain_attn: bfloat16 [1536], P('fsdp'), may hold values from 0.099609375 to 1.8984375
- w_qkv: bfloat16 [1536, 2048], P('fsdp'), may hold values from -0.15625 to 0.15625
- b_qkv: bfloat16 [2048], P('fsdp'), may hold values from -10 to 10
- w_out: bfloat16 [1536, 1536], P('fsdp'), may hold values from -0.625 to 0.625
- gain_mlp: bfloat16 [1536], P('fsdp'), may hold values from 0.099609375 to 1.8984375
- w_gate_up: bfloat16 [1536, 2, 4480], P('fsdp'), may hold values from -0.15625 to 0.15625
- w_down: bfloat16 [4480, 1536], P('fsdp'), may hold values from -0.09375 to 0.09375
- cotangent: bfloat16 [8, 2, 256, 1536], P('ctx', None, 'fsdp'), may hold values from -6 to 6
Outputs:
- block_output: bfloat16 [8, 2, 256, 1536], P('ctx', None, 'fsdp')
- d_tokens: float32 [8, 2, 256, 1536], P('ctx', None, 'fsdp')
- d_gain_attn: float32 [1536], P('fsdp')
- d_w_qkv: float32 [1536, 2048], P('fsdp')
- d_b_qkv: float32 [2048], P('fsdp')
- d_w_out: float32 [1536, 1536], P('fsdp')
- d_gain_mlp: float32 [1536], P('fsdp')
- d_w_gate_up: float32 [1536, 2, 4480], P('fsdp')
- d_w_down: float32 [4480, 1536], P('fsdp')
Inputs may be any that keep to these rules, and one draw needn't show every extreme that they name: Each index of ctx holds stretches pairing[c] and 2 * 8 - 1 - pairing[c] of the sequence.
All inputs are finite; a program needn't handle non-finite values.
Results may differ from a plain program's by a relative error of at most 0.02.
The roundings to bfloat16 on the way count: a program that leaves them out, or rounds other values in their place, can miss the bound.
Values may be sent and summed in bfloat16 or wider, within the bound.
A program may use at most 384 MiB of HBM per device.

v0:
```python
import jax
import jax.numpy as jnp
from jax import lax
from jax.sharding import PartitionSpec as P

D = 1536
HEADS = 12
KV_HEADS = 2
HEAD_DIM = 128
eps = 1e-06
rope_base = 1000000.0


def rope_tables(position):
    half = HEAD_DIM // 2
    inverse = rope_base ** (-(jnp.arange(half, dtype=jnp.float32) * 2.0 / HEAD_DIM))
    angle = position.astype(jnp.float32)[:, None] * inverse[None, :]
    return (jnp.cos(angle)[:, None, :], jnp.sin(angle)[:, None, :])


def rotate(vectors, cosines, sines):
    half = HEAD_DIM // 2
    first, second = (vectors[..., :half], vectors[..., half:])
    return jnp.concatenate([first * cosines - second * sines, second * cosines + first * sines], -1)


def unrotate(grads, cosines, sines):
    half = HEAD_DIM // 2
    first, second = (grads[..., :half], grads[..., half:])
    return jnp.concatenate([first * cosines + second * sines, second * cosines - first * sines], -1)


def rms_scale(values):
    return lax.rsqrt(jnp.mean(values * values, -1, keepdims=True) + eps)


def rms_backward(values, scale_rows, gain, d_normed):
    d_gain = jnp.sum(d_normed * values * scale_rows, 0)
    d_inner = d_normed * gain
    d_values = scale_rows * d_inner - values * scale_rows**3 * jnp.mean(
        d_inner * values, -1, keepdims=True
    )
    return (d_values, d_gain)


def contract_rows(left, right):
    return lax.dot_general(
        left, right, (((0,), (0,)), ((), ())), preferred_element_type=jnp.float32
    )


def contract_cols(left, right):
    return lax.dot_general(
        left, right, (((1,), (1,)), ((), ())), preferred_element_type=jnp.float32
    )


def body(tokens, pairing, gain_attn, w_qkv, b_qkv, w_out, gain_mlp, w_gate_up, w_down, cotangent):
    f32 = jnp.float32
    bf16 = jnp.bfloat16
    half_rows = tokens.shape[2]
    n_ctx = lax.axis_size("ctx")
    n_fsdp = lax.axis_size("fsdp")
    ctx_index = lax.axis_index("ctx")
    fsdp_index = lax.axis_index("fsdp")
    stretch_len = half_rows * n_fsdp
    everyone = n_ctx * n_fsdp
    sequence = 2 * n_ctx * stretch_len
    local_count = 2 * half_rows
    q_width = HEADS * HEAD_DIM
    kv_width = KV_HEADS * HEAD_DIM
    per_group = HEADS // KV_HEADS
    softmax_scale = HEAD_DIM ** (-0.5)
    owner_range = jnp.arange(n_ctx, dtype=jnp.int32)
    own_first = jnp.sum(jnp.where(owner_range == ctx_index, pairing, 0))
    own_second = 2 * n_ctx - 1 - own_first
    inverse_pair = jnp.sum(
        owner_range[:, None] * (pairing[:, None] == owner_range[None, :]).astype(jnp.int32), 0
    )
    offsets = fsdp_index * half_rows + jnp.arange(half_rows, dtype=jnp.int32)
    own_pos = jnp.concatenate(
        [own_first * stretch_len + offsets, own_second * stretch_len + offsets]
    )
    gain_one_w, w_qkv_full, b_qkv_full, w_out_full = (
        lax.all_gather(gain_attn, "fsdp", axis=0, tiled=True),
        lax.all_gather(w_qkv, "fsdp", axis=0, tiled=True),
        lax.all_gather(b_qkv, "fsdp", axis=0, tiled=True),
        lax.all_gather(w_out, "fsdp", axis=0, tiled=True),
    )
    gain_one = gain_one_w.astype(f32)
    inputs = tokens.reshape(local_count, D).astype(f32)
    scale_one = rms_scale(inputs)
    normed1 = (inputs * scale_one * gain_one).astype(bf16)
    qkv = jnp.dot(normed1, w_qkv_full, preferred_element_type=f32) + b_qkv_full.astype(f32)
    cosines, sines = rope_tables(own_pos)
    query16 = rotate(qkv[:, :q_width].reshape(local_count, HEADS, HEAD_DIM), cosines, sines).astype(
        bf16
    )
    key16 = rotate(
        qkv[:, q_width : q_width + kv_width].reshape(local_count, KV_HEADS, HEAD_DIM),
        cosines,
        sines,
    ).astype(bf16)
    value16 = qkv[:, q_width + kv_width :].astype(bf16)
    keys_gathered, values_gathered = (
        lax.all_gather(key16.reshape(2, half_rows, kv_width), ("ctx", "fsdp"), axis=1, tiled=True),
        lax.all_gather(
            value16.reshape(2, half_rows, kv_width), ("ctx", "fsdp"), axis=1, tiled=True
        ),
    )

    def by_position(gathered):
        laid = gathered.reshape(2, n_ctx, stretch_len, kv_width)
        ordered = jnp.concatenate(
            [
                jnp.take(laid[0], inverse_pair, axis=0),
                jnp.take(laid[1], inverse_pair[::-1], axis=0),
            ],
            0,
        )
        return ordered.reshape(sequence, KV_HEADS, HEAD_DIM)

    keys_sorted = by_position(keys_gathered)
    values_sorted = by_position(values_gathered)
    query_halves = query16.reshape(2, half_rows, KV_HEADS, per_group, HEAD_DIM)
    pos_halves = own_pos.reshape(2, half_rows)
    stretch_ids = (own_first, own_second)
    key_iota = jnp.arange(stretch_len, dtype=jnp.int32)

    def masked_scores(query_half, pos_half, key_block, start):
        scores = (
            jnp.einsum("tkgd,skd->kgts", query_half, key_block, preferred_element_type=f32)
            * softmax_scale
        )
        visible = (start + key_iota)[None, None, None, :] <= pos_half[None, None, :, None]
        return (jnp.where(visible, scores, -1e30), visible)

    lse_parts = []
    att_parts = []
    for which in range(2):
        forward_query_half = query_halves[which]
        forward_pos_half = pos_halves[which]
        forward_stretch_id = stretch_ids[which]

        def stat_step(block, carry):
            running_max, totals = carry
            start = block * stretch_len
            key_block = lax.dynamic_slice_in_dim(keys_sorted, start, stretch_len, 0)
            scores, visible = masked_scores(forward_query_half, forward_pos_half, key_block, start)
            new_max = jnp.maximum(running_max, jnp.max(scores, -1))
            weights = jnp.where(visible, jnp.exp(scores - new_max[..., None]), 0.0)
            totals = totals * jnp.exp(running_max - new_max) + jnp.sum(weights, -1)
            return (new_max, totals)

        start_max = jnp.full((KV_HEADS, per_group, half_rows), -1e30, f32)
        start_tot = jnp.zeros((KV_HEADS, per_group, half_rows), f32)
        running_max, totals = lax.fori_loop(
            0, forward_stretch_id + 1, stat_step, (start_max, start_tot)
        )
        lse_half = running_max + jnp.log(totals)

        def value_step(block, accumulated):
            start = block * stretch_len
            key_block = lax.dynamic_slice_in_dim(keys_sorted, start, stretch_len, 0)
            value_block = lax.dynamic_slice_in_dim(values_sorted, start, stretch_len, 0)
            scores, visible = masked_scores(forward_query_half, forward_pos_half, key_block, start)
            probs16 = jnp.where(visible, jnp.exp(scores - lse_half[..., None]), 0.0).astype(bf16)
            return accumulated + jnp.einsum(
                "kgts,skd->kgtd", probs16, value_block, preferred_element_type=f32
            )

        start_acc = jnp.zeros((KV_HEADS, per_group, half_rows, HEAD_DIM), f32)
        accumulated = lax.fori_loop(0, forward_stretch_id + 1, value_step, start_acc)
        lse_half, accumulated = (lse_half, accumulated)
        lse_parts.append(lse_half)
        att_parts.append(accumulated)
    attended = jnp.concatenate(att_parts, 2)
    attended16 = attended.transpose(2, 0, 1, 3).reshape(local_count, q_width).astype(bf16)
    hidden = inputs + jnp.dot(attended16, w_out_full, preferred_element_type=f32)
    gain_two_w, w_gu_full, w_down_full = (
        lax.all_gather(gain_mlp, "fsdp", axis=0, tiled=True),
        lax.all_gather(w_gate_up, "fsdp", axis=0, tiled=True),
        lax.all_gather(w_down, "fsdp", axis=0, tiled=True),
    )
    gain_two = gain_two_w.astype(f32)
    scale_two = rms_scale(hidden)
    normed2 = (hidden * scale_two * gain_two).astype(bf16)
    gate_up = jnp.einsum("td,def->tef", normed2, w_gu_full, preferred_element_type=f32)
    gate_val = gate_up[:, 0]
    up_val = gate_up[:, 1]
    act16 = (jax.nn.silu(gate_val) * up_val).astype(bf16)
    result = hidden + jnp.dot(act16, w_down_full, preferred_element_type=f32)
    block_output = result.astype(bf16).reshape(tokens.shape)
    gain_two_back, w_gu_back, w_down_back = (
        lax.all_gather(gain_mlp, "fsdp", axis=0, tiled=True),
        lax.all_gather(w_gate_up, "fsdp", axis=0, tiled=True),
        lax.all_gather(w_down, "fsdp", axis=0, tiled=True),
    )
    cot = cotangent.reshape(local_count, D)
    d_act = contract_cols(cot, w_down_back)
    d_w_down = contract_rows(act16, cot)
    sigmoid_gate = jax.nn.sigmoid(gate_val)
    d_gate = d_act * up_val * sigmoid_gate * (1.0 + gate_val * (1.0 - sigmoid_gate))
    d_up = d_act * gate_val * sigmoid_gate
    d_gu16 = jnp.stack([d_gate, d_up], 1).astype(bf16)
    d_w_gate_up = jnp.einsum("td,tef->def", normed2, d_gu16, preferred_element_type=f32)
    d_normed2 = jnp.einsum("tef,def->td", d_gu16, w_gu_back, preferred_element_type=f32)
    d_hidden_norm, d_gain_two = rms_backward(
        hidden, scale_two, gain_two_back.astype(f32), d_normed2
    )
    mlp_shards = (
        lax.psum_scatter(d_gain_two, "fsdp", scatter_dimension=0, tiled=True),
        lax.psum_scatter(d_w_gate_up, "fsdp", scatter_dimension=0, tiled=True),
        lax.psum_scatter(d_w_down, "fsdp", scatter_dimension=0, tiled=True),
    )
    gain_two_shard, gate_up_shard, down_shard = mlp_shards
    d_gain_mlp, d_w_gate_up_out, d_w_down_out = lax.psum(
        (gain_two_shard, gate_up_shard, down_shard), "ctx"
    )
    d_hidden = cot.astype(f32) + d_hidden_norm
    d_hidden16 = d_hidden.astype(bf16)
    gain_one_back, w_qkv_back, b_unused, w_out_back = (
        lax.all_gather(gain_attn, "fsdp", axis=0, tiled=True),
        lax.all_gather(w_qkv, "fsdp", axis=0, tiled=True),
        lax.all_gather(b_qkv, "fsdp", axis=0, tiled=True),
        lax.all_gather(w_out, "fsdp", axis=0, tiled=True),
    )
    d_w_out = contract_rows(attended16, d_hidden16)
    d_attended16 = contract_cols(d_hidden16, w_out_back).astype(bf16)
    delta = jnp.sum(
        d_attended16.astype(f32).reshape(local_count, HEADS, HEAD_DIM)
        * attended16.astype(f32).reshape(local_count, HEADS, HEAD_DIM),
        -1,
    )
    delta = delta.reshape(local_count, KV_HEADS, per_group).transpose(1, 2, 0)
    d_att_halves = d_attended16.reshape(2, half_rows, KV_HEADS, per_group, HEAD_DIM)
    zero_kv = jnp.zeros((sequence, KV_HEADS, HEAD_DIM), f32)
    buffers = (zero_kv, zero_kv)
    dq_parts = []
    for which in range(2):
        span = slice(which * half_rows, (which + 1) * half_rows)
        backward_query_half = query_halves[which]
        backward_pos_half = pos_halves[which]
        backward_lse_half = lse_parts[which]
        delta_half = delta[:, :, span]
        d_att_half = d_att_halves[which]

        def step(block, carry):
            d_query, d_key_buf, d_value_buf = carry
            start = block * stretch_len
            key_block = lax.dynamic_slice_in_dim(keys_sorted, start, stretch_len, 0)
            value_block = lax.dynamic_slice_in_dim(values_sorted, start, stretch_len, 0)
            scores, visible = masked_scores(
                backward_query_half, backward_pos_half, key_block, start
            )
            probs = jnp.where(visible, jnp.exp(scores - backward_lse_half[..., None]), 0.0)
            probs16 = probs.astype(bf16)
            d_probs = jnp.einsum(
                "tkgd,skd->kgts", d_att_half, value_block, preferred_element_type=f32
            )
            d_scores16 = (probs * (d_probs - delta_half[..., None])).astype(bf16)
            d_query = d_query + softmax_scale * jnp.einsum(
                "kgts,skd->kgtd", d_scores16, key_block, preferred_element_type=f32
            )
            d_key_block = softmax_scale * jnp.einsum(
                "kgts,tkgd->skd", d_scores16, backward_query_half, preferred_element_type=f32
            )
            d_value_block = jnp.einsum(
                "kgts,tkgd->skd", probs16, d_att_half, preferred_element_type=f32
            )
            d_key_buf = lax.dynamic_update_slice_in_dim(
                d_key_buf,
                lax.dynamic_slice_in_dim(d_key_buf, start, stretch_len, 0) + d_key_block,
                start,
                0,
            )
            d_value_buf = lax.dynamic_update_slice_in_dim(
                d_value_buf,
                lax.dynamic_slice_in_dim(d_value_buf, start, stretch_len, 0) + d_value_block,
                start,
                0,
            )
            return (d_query, d_key_buf, d_value_buf)

        zero_query = jnp.zeros((KV_HEADS, per_group, half_rows, HEAD_DIM), f32)
        d_query_half, d_key_buf, d_value_buf = lax.fori_loop(
            0, stretch_ids[which] + 1, step, (zero_query, buffers[0], buffers[1])
        )
        buffers = (d_key_buf, d_value_buf)
        dq_parts.append(d_query_half)
    d_query = jnp.concatenate(dq_parts, 2)

    def by_device(buffer):
        laid = buffer.reshape(2 * n_ctx, stretch_len, kv_width)
        ordered = jnp.stack(
            [jnp.take(laid, pairing, axis=0), jnp.take(laid, 2 * n_ctx - 1 - pairing, axis=0)], 0
        )
        return ordered.reshape(2, everyone * half_rows, kv_width)

    d_keys_own, d_values_own = (
        lax.psum_scatter(by_device(buffers[0]), ("ctx", "fsdp"), scatter_dimension=1, tiled=True),
        lax.psum_scatter(by_device(buffers[1]), ("ctx", "fsdp"), scatter_dimension=1, tiled=True),
    )
    d_query = unrotate(
        d_query.transpose(2, 0, 1, 3).reshape(local_count, HEADS, HEAD_DIM), cosines, sines
    ).reshape(local_count, q_width)
    d_keys = unrotate(d_keys_own.reshape(local_count, KV_HEADS, HEAD_DIM), cosines, sines).reshape(
        local_count, kv_width
    )
    d_qkv = jnp.concatenate([d_query, d_keys, d_values_own.reshape(local_count, kv_width)], 1)
    d_b_qkv = jnp.sum(d_qkv, 0)
    d_qkv16 = d_qkv.astype(bf16)
    d_w_qkv = contract_rows(normed1, d_qkv16)
    d_normed1 = contract_cols(d_qkv16, w_qkv_back)
    d_input_norm, d_gain_one = rms_backward(inputs, scale_one, gain_one_back.astype(f32), d_normed1)
    attn_shards = (
        lax.psum_scatter(d_gain_one, "fsdp", scatter_dimension=0, tiled=True),
        lax.psum_scatter(d_w_qkv, "fsdp", scatter_dimension=0, tiled=True),
        lax.psum_scatter(d_b_qkv, "fsdp", scatter_dimension=0, tiled=True),
        lax.psum_scatter(d_w_out, "fsdp", scatter_dimension=0, tiled=True),
    )
    gain_one_shard, qkv_shard, bias_shard, out_shard = attn_shards
    d_gain_attn, d_w_qkv_out, d_b_qkv_out, d_w_out_out = lax.psum(
        (gain_one_shard, qkv_shard, bias_shard, out_shard), "ctx"
    )
    d_tokens = (d_hidden + d_input_norm).reshape(tokens.shape)
    return (
        block_output,
        d_tokens,
        d_gain_attn,
        d_w_qkv_out,
        d_b_qkv_out,
        d_w_out_out,
        d_gain_mlp,
        d_w_gate_up_out,
        d_w_down_out,
    )


def solution(mesh):
    placed = (
        P("ctx", None, "fsdp", None),
        P(),
        P("fsdp"),
        P("fsdp", None),
        P("fsdp"),
        P("fsdp", None),
        P("fsdp"),
        P("fsdp", None, None),
        P("fsdp", None),
        P("ctx", None, "fsdp", None),
    )
    return jax.shard_map(
        body,
        mesh=mesh,
        in_specs=placed,
        out_specs=(
            P("ctx", None, "fsdp", None),
            P("ctx", None, "fsdp", None),
            P("fsdp"),
            P("fsdp", None),
            P("fsdp"),
            P("fsdp", None),
            P("fsdp"),
            P("fsdp", None, None),
            P("fsdp", None),
        ),
        check_vma=False,
    )
```

profile of v0, /device:TPU:0, one launch (start us, length us, event | category | flops | bytes accessed | tf_op | source)
XLA Modules:
  0.0 2571.1 jit_solution(16829387691928757474)
XLA Ops:
  8.7 6.2 all-gather
  16.8 5.5 all-gather.1
  22.5 36.2 %all-gather.10.cloned.1.call-done = bf16[1536,2048]{1,0:T(8,128)(2,1)} async-done(((bf16[384,2048]{1,0:T(8,128)(2,1)}), bf16[1536,2048]{1,0:T(8,128)(2,1)}) %all-gather.10.cloned.1.call-update) | async-done | bytes 6291472 | tf_op jit(solution)/shard_map/all_gather | solution.py:86
  58.7 3.8 convolution_add_fusion.2
  67.6 6.6 copy.160
  75.7 5.2 all-gather.2
  84.4 35.4 %all-gather.14.cloned.1.call-done = bf16[2,2048,256]{2,1,0:T(8,128)(2,1)} async-done(((bf16[2,64,256]{2,1,0:T(8,128)(2,1)}), bf16[2,2048,256]{2,1,0:T(8,128)(2,1)}) %all-gather.14.cloned.1.call-update) | async-done | bytes 2097168 | tf_op jit(solution)/shard_map/all_gather | solution.py:107
  119.8 2.6 fusion.182
  123.0 55.6 %all-gather.12.cloned.1.call-done = bf16[2,2048,256]{2,1,0:T(8,128)(2,1)} async-done(((bf16[2,64,256]{2,1,0:T(8,128)(2,1)}), bf16[2,2048,256]{2,1,0:T(8,128)(2,1)}) %all-gather.12.cloned.1.call-update) | async-done | bytes 2097168 | tf_op jit(solution)/shard_map/all_gather | solution.py:106
  178.7 2.6 fusion.183
  184.8 2.9 gather_fusion
  187.7 2.8 broadcast_select_fusion.4
  191.9 2.0 reshape.620
  193.9 2.0 copy.150
  197.6 4.0 reshape.621
  201.5 3.2 copy.152
  204.7 13.9 while.80
  218.6 25.0 while.81
  248.3 2.1 maximum_convert_fusion
  250.4 3.4 multiply_reduce_fusion.2
  253.8 131.9 %all-gather.18.cloned.1.call-done = bf16[1536,2,4480]{2,0,1:T(8,128)(2,1)} async-done(((bf16[384,2,4480]{2,0,1:T(8,128)(2,1)}), bf16[1536,2,4480]{2,0,1:T(8,128)(2,1)}) %all-gather.18.cloned.1.call-update) | async-done | bytes 27525136 | tf_op jit(solution)/shard_map/all_gather | solution.py:182
  385.7 16.4 fusion.167
  402.1 73.9 %all-gather.20.cloned.1.call-done = bf16[4480,1536]{1,0:T(8,128)(2,1)} async-done(((bf16[1120,1536]{1,0:T(8,128)(2,1)}), bf16[4480,1536]{1,0:T(8,128)(2,1)}) %all-gather.20.cloned.1.call-update) | async-done | bytes 13762576 | tf_op jit(solution)/shard_map/all_gather | solution.py:183
  476.0 11.9 fusion.149
  487.8 16.1 multiply_reduce_fusion
  505.3 4.3 convolution_convert_fusion
  512.4 2.3 broadcast_in_dim.144
  514.6 2.3 broadcast_in_dim.144.clone
  516.9 7.8 while.82
  522.6 2.0 fusion.284
  525.0 123.9 %while.83 = (s32[]{:T(128)}, f32[2,6,64,128]{3,2,1,0:T(8,128)S(1)}, f32[4096,2,128]{2,0,1:T(8,128)}, f32[4096,2,128]{2,0,1:T(8,128)}, s32[]{:T(128)}, /*index=5*...) while((s32[]{:T(128)}, f32[2,6,64,128]{3,2,1,0:T(8,128)S(1)}, ...), condition=%wide.region_21.23_spmd.clone, body=%wide.region_20.22_spmd.clone.sunk | while | flops 253641088 | bytes 6595315 | solution.py:286
  530.8 2.0 fusion.299
  546.3 2.0 fusion.299
  623.6 2.0 fusion.299
  631.4 2.0 fusion.299
  648.9 9.1 copy.209
  658.0 6.4 reshape.625
  664.4 8.7 copy.211
  673.1 6.5 reshape.626
  679.6 4.3 gather_fusion.5
  683.9 4.3 gather_fusion.7
  688.2 4.3 gather_fusion.4
  692.5 4.3 gather_fusion.6
  696.8 4.2 broadcast_select_fusion.2
  702.9 2.3 pad_maximum_fusion.1
  705.2 4.5 pad_maximum_fusion
  709.8 5.0 fusion.163
  715.8 131.8 %reduce-scatter.9.cloned.1.call-done = f32[2,64,256]{2,1,0:T(8,128)} async-done(((f32[2,2048,256]{2,1,0:T(8,128)}), f32[2,64,256]{2,1,0:T(8,128)}) %reduce-scatter.9.cloned.1.call-update) | async-done | bytes 131088 | tf_op jit(solution)/shard_map/reduce_scatter | solution.py:302
  848.5 139.4 %reduce-scatter.7.cloned.1.call-done = f32[2,64,256]{2,1,0:T(8,128)} async-done(((f32[2,2048,256]{2,1,0:T(8,128)}), f32[2,64,256]{2,1,0:T(8,128)}) %reduce-scatter.7.cloned.1.call-update) | async-done | bytes 131088 | tf_op jit(solution)/shard_map/reduce_scatter | solution.py:301
  989.5 8.6 fusion.176
  999.2 14.8 fusion.145
  1015.3 23.1 fusion.143
  1038.5 25.8 %reduce-scatter.13.cloned.1.call-done = f32[384,1536]{1,0:T(8,128)} async-done(((f32[1536,1536]{1,0:T(8,128)}), f32[384,1536]{1,0:T(8,128)}) %reduce-scatter.13.cloned.1.call-update) | async-done | bytes 2359312 | tf_op jit(solution)/shard_map/reduce_scatter | solution.py:320
  1064.3 102.6 %reduce-scatter.11.cloned.1.call-done = f32[384,2048]{1,0:T(8,128)} async-done(((f32[1536,2048]{1,0:T(8,128)}), f32[384,2048]{1,0:T(8,128)}) %reduce-scatter.11.cloned.1.call-update) | async-done | bytes 3145744 | tf_op jit(solution)/shard_map/reduce_scatter | solution.py:318
  1167.0 200.4 %reduce-scatter.17.cloned.1.call-done = f32[1120,1536]{1,0:T(8,128)} async-done(((f32[4480,1536]{1,0:T(8,128)}), f32[1120,1536]{1,0:T(8,128)}) %reduce-scatter.17.cloned.1.call-update) | async-done | bytes 6881296 | tf_op jit(solution)/shard_map/reduce_scatter | solution.py:214
  1367.3 380.5 %reduce-scatter.15.cloned.1.call-done = f32[384,2,4480]{2,0,1:T(8,128)} async-done(((f32[1536,2,4480]{2,0,1:T(8,128)}), f32[384,2,4480]{2,0,1:T(8,128)}) %reduce-scatter.15.cloned.1.call-update) | async-done | bytes 13762576 | tf_op jit(solution)/shard_map/reduce_scatter | solution.py:213
  1750.9 9.4 fusion.132
  1760.7 3.7 fusion.159
  1764.5 11.6 all-reduce.5
  1776.3 23.8 all-reduce.3
  1800.7 2.4 fusion.156
  1803.1 720.3 %all-reduce.8.cloned.1.call-done = (f32[384,2048]{1,0:T(8,128)}, f32[384,1536]{1,0:T(8,128)}, f32[384,2,4480]{2,0,1:T(8,128)}, f32[1120,1536]{1,0:T(8,128)}) async-done(((f32[384,2048]{1,0:T(8,128)}, f32[384,1536]{1,0:T(8,128)}, f32[384,2,4480]{2,0,1:T(8,128)}, f32[1120,1536]{1,0:T(8,128)}), (f32[384,2048]{1,0:T(8,128)}, f32[384,1536]{1,0:T(8,128)}, f32[384,2,4480]{2,0,1:T(8,128)}, ...) | async-done | bytes 26148880 | tf_op jit(solution)/shard_map/psum | solution.py:323
  2523.4 33.1 %copy.180 = f32[384,2,4480]{2,1,0:T(2,128)} copy(f32[384,2,4480]{2,0,1:T(8,128)} %get-tuple-element.961) | data formatting | bytes 27525120
  2561.4 2.9 copy.277
  (540 shorter events, 202.8 us)
Async XLA Ops:
  7.2 15.1 copy-start.5
  7.2 51.5 %all-gather.10.cloned.1.call-start = ((), (), s32[]{:S(2)}) async-start(), calls=%async_computation.6 | async-start | bytes 7864320 | tf_op jit(solution)/shard_map/all_gather | solution.py:86
  7.9 111.9 %all-gather.14.cloned.1.call-start = ((), (), s32[]{:S(2)}) async-start(), calls=%async_computation.8 | async-start | bytes 2162688 | tf_op jit(solution)/shard_map/all_gather | solution.py:107
  14.9 43.8 %copy-start.28 = (f32[1536]{0:T(1024)}, f32[1536]{0:T(1024)S(1)}, u32[]{:S(2)}) copy-start(f32[1536]{0:T(1024)S(1)} %reshape.584) | copy-start | bytes 18436
  16.1 42.6 %copy-start.32 = (f32[128]{0:T(128)}, f32[128]{0:T(128)S(1)}, u32[]{:S(2)}) copy-start(f32[128]{0:T(128)S(1)} %rsqrt.26) | copy-start | bytes 1540
  22.5 40.0 %copy-start.11 = (bf16[128,1536]{1,0:T(8,128)(2,1)}, bf16[128,1536]{1,0:T(8,128)(2,1)S(1)}, u32[]{:S(2)}) copy-start(bf16[128,1536]{1,0:T(8,128)(2,1)S(1)} %fusion.153) | copy-start | bytes 1179652
  58.7 4.5 copy-start.37
  63.1 115.5 %all-gather.12.cloned.1.call-start = ((), (), s32[]{:S(2)}) async-start(), calls=%async_computation.7 | async-start | bytes 2162688 | tf_op jit(solution)/shard_map/all_gather | solution.py:106
  65.5 18.3 copy-start.24
  65.5 18.3 copy-start.26
  65.7 8.5 copy-start.22
  67.0 183.5 %all-gather.16.cloned.1.call-start = ((), (), s32[]{:S(2)}) async-start(), calls=%async_computation.9 | async-start | bytes 5898240 | tf_op jit(solution)/shard_map/all_gather | solution.py:88
  67.5 318.2 %all-gather.18.cloned.1.call-start = ((), (), s32[]{:S(2)}) async-start(), calls=%async_computation.10 | async-start | bytes 34406400 | tf_op jit(solution)/shard_map/all_gather | solution.py:182
  74.2 1.4 copy-start.38
  74.2 401.7 %all-gather.20.cloned.1.call-start = ((), (), s32[]{:S(2)}) async-start(), calls=%async_computation.11 | async-start | bytes 17203200 | tf_op jit(solution)/shard_map/all_gather | solution.py:183
  74.8 772.7 %reduce-scatter.9.cloned.1.call-start = ((), (), s32[]{:S(2)}) async-start(), calls=%async_computation.13 | async-start | bytes 4325376 | tf_op jit(solution)/shard_map/reduce_scatter | solution.py:302
  187.7 2.8 copy-start.13
  193.9 2.0 copy-start.14
  193.9 2.2 copy-start.15
  247.2 3.2 copy-start.4
  247.2 6.5 copy-start.30
  385.7 90.2 %copy-start.18 = (bf16[1,2,64,1536]{3,2,1,0:T(8,128)(2,1)S(1)}, bf16[1,2,64,1536]{3,2,1,0:T(8,128)(2,1)}, u32[]{:S(2)}) copy-start(bf16[1,2,64,1536]{3,2,1,0:T(8,128)(2,1)} %param.35) | copy-start | bytes 1179652
  487.8 16.1 copy-start.20
  505.3 204.5 %copy-start.2 = (f32[128,1536]{1,0:T(8,128)}, f32[128,1536]{1,0:T(8,128)S(1)}, u32[]{:S(2)}) copy-start(f32[128,1536]{1,0:T(8,128)S(1)} %subtract_add_fusion) | copy-start | bytes 2359300
  509.6 1.4 copy-start.9
  514.6 2.3 copy-start.31
  692.5 4.3 copy-start.36
  696.8 4.2 copy-start.7
  696.8 4.2 copy-start.8
  696.8 4.2 copy-start.35
  705.2 282.7 %reduce-scatter.7.cloned.1.call-start = ((), (), s32[]{:S(2)}) async-start(), calls=%async_computation.12 | async-start | bytes 4325376 | tf_op jit(solution)/shard_map/reduce_scatter | solution.py:301
  709.7 354.6 %reduce-scatter.13.cloned.1.call-start = ((), (), s32[]{:S(2)}) async-start(), calls=%async_computation.15 | async-start | bytes 11796480 | tf_op jit(solution)/shard_map/reduce_scatter | solution.py:320
  714.8 0.8 copy-start.25
  714.8 0.8 copy-start.27
  714.8 452.1 %reduce-scatter.11.cloned.1.call-start = ((), (), s32[]{:S(2)}) async-start(), calls=%async_computation.14 | async-start | bytes 15728640 | tf_op jit(solution)/shard_map/reduce_scatter | solution.py:318
  714.9 273.9 %copy-start.23 = (f32[128,64]{1,0:T(8,128)S(1)}, f32[128,64]{1,0:T(8,128)}, u32[]{:S(2)}) copy-start(f32[128,64]{1,0:T(8,128)} %copy-done.22) | copy-start | bytes 98308
  715.6 273.9 %copy-start.12 = (bf16[128,1536]{1,0:T(8,128)(2,1)S(1)}, bf16[128,1536]{1,0:T(8,128)(2,1)}, u32[]{:S(2)}) copy-start(bf16[128,1536]{1,0:T(8,128)(2,1)} %copy-done.11) | copy-start | bytes 1179652
  715.8 282.3 %copy-start = (f32[128,12,128]{0,2,1:T(8,128)}, f32[128,12,128]{0,2,1:T(8,128)S(1)}, u32[]{:S(2)}) copy-start(f32[128,12,128]{0,2,1:T(8,128)S(1)} %pad_maximum_fusion.8) | copy-start | bytes 2359300
  998.1 1.1 copy-start.19
  998.1 369.2 %reduce-scatter.17.cloned.1.call-start = ((), (), s32[]{:S(2)}) async-start(), calls=%async_computation.17 | async-start | bytes 34406400 | tf_op jit(solution)/shard_map/reduce_scatter | solution.py:214
  1014.0 1.3 copy-start.21
  1014.1 733.8 %reduce-scatter.15.cloned.1.call-start = ((), (), s32[]{:S(2)}) async-start(), calls=%async_computation.16 | async-start | bytes 68812800 | tf_op jit(solution)/shard_map/reduce_scatter | solution.py:213
  1038.5 1485.0 %all-reduce.8.cloned.1.call-start = ((), (), s32[]{:S(2)}) async-start(), calls=%async_computation.18 | async-start | bytes 52297728 | tf_op jit(solution)/shard_map/psum | solution.py:323
  1747.8 0.7 copy-start.39
  1747.8 2.5 copy-start.33
  1747.8 12.8 slice-start
  1750.9 9.4 copy-start.1
  1750.9 9.8 slice-start.1
  1750.9 9.8 copy-start.6
  1750.9 9.8 copy-start.29
  1750.9 9.8 copy-start.34
  1760.7 40.0 %copy-start.3 = (f32[128,1536]{1,0:T(8,128)S(1)}, f32[128,1536]{1,0:T(8,128)}, u32[]{:S(2)}) copy-start(f32[128,1536]{1,0:T(8,128)} %copy-done.2) | copy-start | bytes 2359300
  2523.4 33.1 %copy-start.16 = (f32[384,2048]{1,0:T(8,128)S(1)}, f32[384,2048]{1,0:T(8,128)}, u32[]{:S(2)}) copy-start(f32[384,2048]{1,0:T(8,128)} %get-tuple-element.1648) | copy-start | bytes 9437188
  2523.4 34.8 %copy-start.17 = (f32[384,1536]{1,0:T(8,128)S(1)}, f32[384,1536]{1,0:T(8,128)}, u32[]{:S(2)}) copy-start(f32[384,1536]{1,0:T(8,128)} %get-tuple-element.1650) | copy-start | bytes 7077892
  2556.5 4.9 copy-start.10
Sparse Core Ops, SparseCore 0:
  9.6 49.0 all-gather.9
  63.3 56.4 all-gather.13
  123.3 55.3 all-gather.11
  180.1 36.3 all-gather.15
  218.4 167.2 all-gather.17
  387.1 88.7 all-gather.19
  705.3 142.1 reduce-scatter.8
  849.8 138.0 reduce-scatter.6
  990.5 73.7 reduce-scatter.12
  1067.4 99.5 reduce-scatter.10
  1169.6 197.7 reduce-scatter.16
  1369.8 377.9 reduce-scatter.14
  1752.7 770.6 all-reduce.7
where the time goes:
time: 2580 us; the launch traced here: 2570 us
  waiting for transfers between devices  2040 us (79%)
  matrix products  280 us (11%)
  local copies, waits for them, and re-layouts  138 us (5%)
  blocking collectives  52.2 us (2%)
  other arithmetic  43.2 us (2%)
    psum x1, waiting for transfers between devices, body(): lax.psum((gain_one_shard, qkv_shard, bias_shard, out_shard), 'ctx')  720 us
    reduce_scatter x1, waiting for transfers between devices, body(): lax.psum_scatter(d_w_gate_up, 'fsdp', scatter_dimension=0, tiled=True)  380 us
    reduce_scatter x1, waiting for transfers between devices, body(): lax.psum_scatter(d_w_down, 'fsdp', scatter_dimension=0, tiled=True)  200 us
    reduce_scatter x1, waiting for transfers between devices, body(): lax.psum_scatter(by_device(buffers[0]), ('ctx', 'fsdp'), scatter_dimensio...  139 us
    all_gather x1, waiting for transfers between devices, body(): lax.all_gather(w_gate_up, 'fsdp', axis=0, tiled=True)  132 us
    reduce_scatter x1, waiting for transfers between devices, body(): lax.psum_scatter(by_device(buffers[1]), ('ctx', 'fsdp'), scatter_dimensio...  132 us
    reduce_scatter x1, waiting for transfers between devices, body(): lax.psum_scatter(d_w_qkv, 'fsdp', scatter_dimension=0, tiled=True)  103 us
    all_gather x1, waiting for transfers between devices, body(): lax.all_gather(w_down, 'fsdp', axis=0, tiled=True)  73.9 us
  transfers between devices with their start and end apart: 13, of which 12 were waited for; matrix products, arithmetic and copies ran while one was open for 7% of the time, Pallas kernels for 0%

commit v1 on v0

--- a/solution.py
+++ b/solution.py
@@ -9,6 +9,11 @@
 HEAD_DIM = 128
 eps = 1e-06
 rope_base = 1000000.0
+
+
+def swapped_in(shard, name, dim):
+    stack = jnp.stack([shard] * lax.axis_size(name))
+    return jnp.concatenate(lax.all_to_all(stack, name, 0, 0), axis=dim)
 
 
 def rope_tables(position):
@@ -179,7 +184,7 @@
     hidden = inputs + jnp.dot(attended16, w_out_full, preferred_element_type=f32)
     gain_two_w, w_gu_full, w_down_full = (
         lax.all_gather(gain_mlp, "fsdp", axis=0, tiled=True),
-        lax.all_gather(w_gate_up, "fsdp", axis=0, tiled=True),
+        swapped_in(w_gate_up, "fsdp", 0),
         lax.all_gather(w_down, "fsdp", axis=0, tiled=True),
     )
     gain_two = gain_two_w.astype(f32)

time: 2580 us -> 2800 us (1.085)
  blocking collectives: 52.2 us -> 523 us
  waiting for transfers between devices: 2040 us -> 1740 us
  local copies, waits for them, and re-layouts: 138 us -> 168 us
    all_gather x1, blocking collectives: 5.18 us -> 476 us  [body(): lax.all_gather(gain_mlp, 'fsdp', axis=0, tiled=True)]
    all_gather x1, waiting for transfers between devices: 132 us -> 0.01 us  [body(): lax.all_gather(w_gate_up, 'fsdp', axis=0, tiled=True)]
    all_gather x1, waiting for transfers between devices: 73.9 us -> 0.01 us  [body(): lax.all_gather(w_down, 'fsdp', axis=0, tiled=True)]
    all_gather x1, waiting for transfers between devices: 55.6 us -> 0.02 us  [body(): lax.all_gather(key16.reshape(2, half_rows, kv_width), ('ctx', 'fsdp'), ax...]
    all_gather x1, waiting for transfers between devices: 35.4 us -> 0.02 us  [body(): lax.all_gather(value16.reshape(2, half_rows, kv_width), ('ctx', 'fsdp'),...]
  transfers between devices with their start and end apart: 13 -> 14, of which waited for: 12 -> 8; matrix products, arithmetic and copies ran while one was open for 7% -> 8% of each run, Pallas kernels for 0% -> 0%
where the time goes in v1:
time: 2800 us; the launch traced here: 2780 us
  waiting for transfers between devices  1740 us (62%)
  blocking collectives  523 us (19%)
  matrix products  278 us (10%)
  local copies, waits for them, and re-layouts  168 us (6%)
  other arithmetic  42.4 us (2%)
    psum x1, waiting for transfers between devices, body(): lax.psum((gain_one_shard, qkv_shard, bias_shard, out_shard), 'ctx')  720 us
    all_gather x1, blocking collectives, body(): lax.all_gather(gain_mlp, 'fsdp', axis=0, tiled=True)  476 us
    reduce_scatter x1, waiting for transfers between devices, body(): lax.psum_scatter(d_w_gate_up, 'fsdp', scatter_dimension=0, tiled=True)  380 us
    reduce_scatter x1, waiting for transfers between devices, body(): lax.psum_scatter(d_w_down, 'fsdp', scatter_dimension=0, tiled=True)  200 us
    reduce_scatter x1, waiting for transfers between devices, body(): lax.psum_scatter(by_device(buffers[0]), ('ctx', 'fsdp'), scatter_dimensio...  140 us
    reduce_scatter x1, waiting for transfers between devices, body(): lax.psum_scatter(by_device(buffers[1]), ('ctx', 'fsdp'), scatter_dimensio...  132 us
    reduce_scatter x1, waiting for transfers between devices, body(): lax.psum_scatter(d_w_qkv, 'fsdp', scatter_dimension=0, tiled=True)  103 us
    unnamed x102, local copies, waits for them, and re-layouts  58.7 us
  transfers between devices with their start and end apart: 14, of which 8 were waited for; matrix products, arithmetic and copies ran while one was open for 8% of the time, Pallas kernels for 0%

profile of v1, /device:TPU:0, one launch (start us, length us, event | category | flops | bytes accessed | tf_op | source)
XLA Modules:
  0.0 2782.8 jit_solution(6253447364450887504)
XLA Ops:
  8.7 6.2 all-gather
  16.8 5.5 all-gather.1
  22.5 36.2 %all-gather.10.cloned.1.call-done = bf16[1536,2048]{1,0:T(8,128)(2,1)} async-done(((bf16[384,2048]{1,0:T(8,128)(2,1)}), bf16[1536,2048]{1,0:T(8,128)(2,1)}) %all-gather.10.cloned.1.call-update) | async-done | bytes 6291472 | tf_op jit(solution)/shard_map/all_gather | solution.py:91
  58.7 3.8 convolution_add_fusion.2
  68.2 6.6 copy.165
  74.8 11.2 stack.37
  86.0 8.9 all-to-all-start
  96.5 476.0 %all-gather.2 = bf16[4,1,384]{2,1,0:T(2,128)(2,1)S(1)} all-gather(bf16[1,1,384]{2,1,0:T(2,128)(2,1)S(1)} %reshape.588), channel_id=1, replica_groups=mesh['ctx'=8,'fsdp'=4] {'fsdp'}, dimensions={0}, use_global_device_ids=true | all-gather | bytes 3840 | tf_op jit(solution)/shard_map/all_gather | solution.py:186
  574.8 2.8 fusion.182
  578.3 2.6 fusion.183
  584.4 2.8 gather_fusion
  587.2 2.5 broadcast_select_fusion.4
  591.1 2.0 reshape.626
  593.2 2.2 copy.155
  597.1 4.0 reshape.627
  601.1 3.2 copy.157
  604.3 13.9 while.80
  618.2 24.5 while.81
  647.2 2.1 maximum_convert_fusion
  649.3 3.4 multiply_reduce_fusion.2
  652.8 19.4 copy.166
  672.1 14.7 fusion.167
  686.9 11.8 fusion.149
  698.7 16.1 multiply_reduce_fusion
  716.2 4.3 convolution_convert_fusion
  723.3 2.3 broadcast_in_dim.144
  725.5 2.3 broadcast_in_dim.144.clone
  727.8 7.9 while.82
  736.1 123.7 %while.83 = (s32[]{:T(128)}, f32[2,6,64,128]{3,2,1,0:T(8,128)S(1)}, f32[4096,2,128]{2,0,1:T(8,128)}, f32[4096,2,128]{2,0,1:T(8,128)}, s32[]{:T(128)}, /*index=5*...) while((s32[]{:T(128)}, f32[2,6,64,128]{3,2,1,0:T(8,128)S(1)}, ...), condition=%wide.region_21.23_spmd.clone, body=%wide.region_20.22_spmd.clone.sunk | while | flops 253641088 | bytes 6595315 | solution.py:291
  739.9 2.0 fusion.298
  747.6 2.0 fusion.298
  763.1 2.0 fusion.298
  770.8 2.0 fusion.298
  778.5 2.0 fusion.298
  786.3 2.0 fusion.298
  859.8 8.8 copy.216
  868.6 6.4 reshape.631
  875.0 8.8 copy.218
  883.8 6.4 reshape.632
  890.2 4.3 gather_fusion.5
  894.5 4.3 gather_fusion.7
  898.8 4.2 gather_fusion.4
  903.0 4.2 gather_fusion.6
  907.2 4.2 broadcast_select_fusion.2
  913.3 2.3 pad_maximum_fusion.1
  915.6 4.5 pad_maximum_fusion
  920.2 5.0 fusion.163
  926.3 132.1 %reduce-scatter.9.cloned.1.call-done = f32[2,64,256]{2,1,0:T(8,128)} async-done(((f32[2,2048,256]{2,1,0:T(8,128)}), f32[2,64,256]{2,1,0:T(8,128)}) %reduce-scatter.9.cloned.1.call-update) | async-done | bytes 131088 | tf_op jit(solution)/shard_map/reduce_scatter | solution.py:307
  1059.3 140.3 %reduce-scatter.7.cloned.1.call-done = f32[2,64,256]{2,1,0:T(8,128)} async-done(((f32[2,2048,256]{2,1,0:T(8,128)}), f32[2,64,256]{2,1,0:T(8,128)}) %reduce-scatter.7.cloned.1.call-update) | async-done | bytes 131088 | tf_op jit(solution)/shard_map/reduce_scatter | solution.py:306
  1201.3 8.6 fusion.176
  1210.9 14.8 fusion.145
  1227.0 23.1 fusion.143
  1250.4 25.7 reduce-scatter.13.cloned.1.call-done
  1276.1 102.6 %reduce-scatter.11.cloned.1.call-done = f32[384,2048]{1,0:T(8,128)} async-done(((f32[1536,2048]{1,0:T(8,128)}), f32[384,2048]{1,0:T(8,128)}) %reduce-scatter.11.cloned.1.call-update) | async-done | bytes 3145744 | tf_op jit(solution)/shard_map/reduce_scatter | solution.py:323
  1378.7 200.4 %reduce-scatter.17.cloned.1.call-done = f32[1120,1536]{1,0:T(8,128)} async-done(((f32[4480,1536]{1,0:T(8,128)}), f32[1120,1536]{1,0:T(8,128)}) %reduce-scatter.17.cloned.1.call-update) | async-done | bytes 6881296 | tf_op jit(solution)/shard_map/reduce_scatter | solution.py:219
  1579.1 380.5 %reduce-scatter.15.cloned.1.call-done = f32[384,2,4480]{2,0,1:T(8,128)} async-done(((f32[1536,2,4480]{2,0,1:T(8,128)}), f32[384,2,4480]{2,0,1:T(8,128)}) %reduce-scatter.15.cloned.1.call-update) | async-done | bytes 13762576 | tf_op jit(solution)/shard_map/reduce_scatter | solution.py:218
  1962.7 9.4 fusion.132
  1972.5 3.7 fusion.159
  1976.3 11.6 all-reduce.5
  1988.1 23.6 all-reduce.3
  2012.3 2.4 fusion.156
  2014.7 720.5 %all-reduce.8.cloned.1.call-done = (f32[384,2048]{1,0:T(8,128)}, f32[384,1536]{1,0:T(8,128)}, f32[384,2,4480]{2,0,1:T(8,128)}, f32[1120,1536]{1,0:T(8,128)}) async-done(((f32[384,2048]{1,0:T(8,128)}, f32[384,1536]{1,0:T(8,128)}, f32[384,2,4480]{2,0,1:T(8,128)}, f32[1120,1536]{1,0:T(8,128)}), (f32[384,2048]{1,0:T(8,128)}, f32[384,1536]{1,0:T(8,128)}, f32[384,2,4480]{2,0,1:T(8,128)}, ...) | async-done | bytes 26148880 | tf_op jit(solution)/shard_map/psum | solution.py:328
  2735.2 33.1 %copy.187 = f32[384,2,4480]{2,1,0:T(2,128)} copy(f32[384,2,4480]{2,0,1:T(8,128)} %get-tuple-element.961) | data formatting | bytes 27525120
  2773.2 2.9 copy.284
  (544 shorter events, 199.8 us)
Async XLA Ops:
  7.2 15.1 copy-start.5
  7.2 51.5 %all-gather.10.cloned.1.call-start = ((), (), s32[]{:S(2)}) async-start(), calls=%async_computation.7 | async-start | bytes 7864320 | tf_op jit(solution)/shard_map/all_gather | solution.py:91
  7.9 566.9 %all-gather.14.cloned.1.call-start = ((), (), s32[]{:S(2)}) async-start(), calls=%async_computation.9 | async-start | bytes 2162688 | tf_op jit(solution)/shard_map/all_gather | solution.py:112
  14.9 43.8 %copy-start.26 = (f32[1536]{0:T(1024)}, f32[1536]{0:T(1024)S(1)}, u32[]{:S(2)}) copy-start(f32[1536]{0:T(1024)S(1)} %reshape.590) | copy-start | bytes 18436
  16.1 42.6 %copy-start.32 = (f32[128]{0:T(128)}, f32[128]{0:T(128)S(1)}, u32[]{:S(2)}) copy-start(f32[128]{0:T(128)S(1)} %rsqrt.26) | copy-start | bytes 1540
  22.5 40.0 %copy-start.11 = (bf16[128,1536]{1,0:T(8,128)(2,1)}, bf16[128,1536]{1,0:T(8,128)(2,1)S(1)}, u32[]{:S(2)}) copy-start(bf16[128,1536]{1,0:T(8,128)(2,1)S(1)} %fusion.153) | copy-start | bytes 1179652
  58.7 4.5 copy-start.37
  63.1 515.1 %all-gather.12.cloned.1.call-start = ((), (), s32[]{:S(2)}) async-start(), calls=%async_computation.8 | async-start | bytes 2162688 | tf_op jit(solution)/shard_map/all_gather | solution.py:111
  65.6 2.6 copy-start.22
  65.7 2.5 copy-start.24
  66.9 582.3 %all-gather.16.cloned.1.call-start = ((), (), s32[]{:S(2)}) async-start(), calls=%async_computation.10 | async-start | bytes 5898240 | tf_op jit(solution)/shard_map/all_gather | solution.py:93
  67.5 619.4 %all-gather.18.cloned.1.call-start = ((), (), s32[]{:S(2)}) async-start(), calls=%async_computation.11 | async-start | bytes 17203200 | tf_op jit(solution)/shard_map/all_gather | solution.py:188
  68.1 630.6 %all-gather.20.cloned.1.call-start = ((), (), s32[]{:S(2)}) async-start(), calls=%async_computation.12 | async-start | bytes 34406400 | tf_op jit(solution)/shard_map/all_gather | solution.py:201
  86.0 10.5 copy-start.38
  86.0 566.8 %all-to-all-start = ((bf16[4,384,2,4480]{3,1,2,0:T(8,128)(2,1)}), bf16[4,384,2,4480]{3,1,2,0:T(8,128)(2,1)}, u32[]{:S(2)}, u32[]{:S(2)}) async-start(bf16[4,384,2,4480]{3,1,2,0:T(8,128)(2,1)} %stack.37), calls=%async_computation | async-start | bytes 55050240 | tf_op jit(solution)/shard_map/all_to_all | solution.py:16
  94.9 963.4 %reduce-scatter.9.cloned.1.call-start = ((), (), s32[]{:S(2)}) async-start(), calls=%async_computation.14 | async-start | bytes 4325376 | tf_op jit(solution)/shard_map/reduce_scatter | solution.py:307
  587.2 2.5 copy-start.13
  593.2 2.2 copy-start.14
  593.2 2.4 copy-start.15
  642.7 0.9 copy-start.28
  646.1 3.2 copy-start.4
  646.1 6.6 copy-start.30
  672.1 14.7 copy-start.18
  698.7 16.1 copy-start.20
  716.2 204.0 %copy-start.2 = (f32[128,1536]{1,0:T(8,128)}, f32[128,1536]{1,0:T(8,128)S(1)}, u32[]{:S(2)}) copy-start(f32[128,1536]{1,0:T(8,128)S(1)} %subtract_add_fusion) | copy-start | bytes 2359300
  720.5 1.4 copy-start.9
  725.5 2.3 copy-start.31
  727.8 8.3 copy-start.29
  903.0 4.2 copy-start.36
  907.2 4.2 copy-start.7
  907.2 4.2 copy-start.8
  907.2 4.2 copy-start.35
  915.6 284.1 %reduce-scatter.7.cloned.1.call-start = ((), (), s32[]{:S(2)}) async-start(), calls=%async_computation.13 | async-start | bytes 4325376 | tf_op jit(solution)/shard_map/reduce_scatter | solution.py:306
  920.2 355.9 %reduce-scatter.13.cloned.1.call-start = ((), (), s32[]{:S(2)}) async-start(), calls=%async_computation.16 | async-start | bytes 11796480 | tf_op jit(solution)/shard_map/reduce_scatter | solution.py:325
  925.2 453.5 %reduce-scatter.11.cloned.1.call-start = ((), (), s32[]{:S(2)}) async-start(), calls=%async_computation.15 | async-start | bytes 15728640 | tf_op jit(solution)/shard_map/reduce_scatter | solution.py:323
  925.8 274.9 %copy-start.23 = (f32[128,64]{1,0:T(8,128)S(1)}, f32[128,64]{1,0:T(8,128)}, u32[]{:S(2)}) copy-start(f32[128,64]{1,0:T(8,128)} %copy-done.22) | copy-start | bytes 98308
  925.8 274.9 %copy-start.25 = (f32[128,64]{1,0:T(8,128)S(1)}, f32[128,64]{1,0:T(8,128)}, u32[]{:S(2)}) copy-start(f32[128,64]{1,0:T(8,128)} %copy-done.24) | copy-start | bytes 98308
  926.1 275.2 %copy-start.12 = (bf16[128,1536]{1,0:T(8,128)(2,1)S(1)}, bf16[128,1536]{1,0:T(8,128)(2,1)}, u32[]{:S(2)}) copy-start(bf16[128,1536]{1,0:T(8,128)(2,1)} %copy-done.11) | copy-start | bytes 1179652
  926.2 283.6 %copy-start = (f32[128,12,128]{0,2,1:T(8,128)}, f32[128,12,128]{0,2,1:T(8,128)S(1)}, u32[]{:S(2)}) copy-start(f32[128,12,128]{0,2,1:T(8,128)S(1)} %pad_maximum_fusion.8) | copy-start | bytes 2359300
  1209.8 1.1 copy-start.19
  1209.9 369.2 %reduce-scatter.17.cloned.1.call-start = ((), (), s32[]{:S(2)}) async-start(), calls=%async_computation.18 | async-start | bytes 34406400 | tf_op jit(solution)/shard_map/reduce_scatter | solution.py:219
  1225.7 1.3 copy-start.21
  1225.7 733.9 %reduce-scatter.15.cloned.1.call-start = ((), (), s32[]{:S(2)}) async-start(), calls=%async_computation.17 | async-start | bytes 68812800 | tf_op jit(solution)/shard_map/reduce_scatter | solution.py:218
  1250.1 1485.0 %all-reduce.8.cloned.1.call-start = ((), (), s32[]{:S(2)}) async-start(), calls=%async_computation.19 | async-start | bytes 52297728 | tf_op jit(solution)/shard_map/psum | solution.py:328
  1959.6 0.7 copy-start.39
  1959.6 2.5 copy-start.33
  1959.6 12.8 slice-start
  1962.7 9.4 copy-start.1
  1962.7 9.8 slice-start.1
  1962.7 9.8 copy-start.6
  1962.7 9.8 copy-start.27
  1962.7 9.8 copy-start.34
  1972.5 39.8 %copy-start.3 = (f32[128,1536]{1,0:T(8,128)S(1)}, f32[128,1536]{1,0:T(8,128)}, u32[]{:S(2)}) copy-start(f32[128,1536]{1,0:T(8,128)} %copy-done.2) | copy-start | bytes 2359300
  2735.2 33.1 %copy-start.16 = (f32[384,2048]{1,0:T(8,128)S(1)}, f32[384,2048]{1,0:T(8,128)}, u32[]{:S(2)}) copy-start(f32[384,2048]{1,0:T(8,128)} %get-tuple-element.1648) | copy-start | bytes 9437188
  2735.2 34.8 %copy-start.17 = (f32[384,1536]{1,0:T(8,128)S(1)}, f32[384,1536]{1,0:T(8,128)}, u32[]{:S(2)}) copy-start(f32[384,1536]{1,0:T(8,128)} %get-tuple-element.1650) | copy-start | bytes 7077892
  2768.2 4.9 copy-start.10
Sparse Core Ops, SparseCore 0:
  9.6 49.0 all-gather.9
  63.3 58.7 all-gather.13
  125.5 58.0 all-gather.11
  185.0 61.7 all-gather.15
  248.2 162.5 all-gather.17
  412.9 237.7 all-gather.19
  915.7 142.5 reduce-scatter.8
  1061.2 138.4 reduce-scatter.6
  1202.2 73.7 reduce-scatter.12
  1279.1 99.5 reduce-scatter.10
  1381.3 197.7 reduce-scatter.16
  1581.6 377.9 reduce-scatter.14
  1964.5 770.6 all-reduce.7
